TPU v7x, 32 devices: a whole 2x2x4 slice. The times are simulated.
32 devices in a mesh: batch: 8 (over y, x, core), tensor: 4 (over z).
Axes of the slice: x: 2, y: 2, z: 4, core: 2. Of those that a mesh axis runs over, the one named last changes fastest.
Arguments:
- hidden_in: bfloat16 [32, 512, 768], P(('batch', 'tensor')), may hold values from -6 to 6
- segment_ids: int32 [32, 512], P('batch'), may hold values from 0 to 7, never falling along the last dimension, each value on 1 to 128 neighbouring positions
- query_weight: bfloat16 [768, 768], P(None, 'tensor'), may hold values from -0.21875 to 0.21875
- query_bias: float32 [768], P('tensor'), may hold values from -3 to 3
- key_weight: bfloat16 [768, 768], P(None, 'tensor'), may hold values from -0.21875 to 0.21875
- value_weight: bfloat16 [768, 768], P(None, 'tensor'), may hold values from -0.21875 to 0.21875
- value_bias: float32 [768], P('tensor'), may hold values from -3 to 3
- out_weight: bfloat16 [768, 768], P('tensor'), may hold values from -1.25 to 1.25
- out_bias: float32 [768], replicated, may hold values from -3 to 3
- attn_gain: float32 [768], replicated, may hold values from 0.5 to 1.5
- attn_shift: float32 [768], replicated, may hold values from -3 to 3
- up_weight: bfloat16 [768, 3072], P(None, 'tensor'), may hold values from -0.21875 to 0.21875
- up_bias: float32 [3072], P('tensor'), may hold values from -3 to 3
- down_weight: bfloat16 [3072, 768], P('tensor'), may hold values from -0.109375 to 0.109375
- down_bias: float32 [768], replicated, may hold values from -3 to 3
- ffn_gain: float32 [768], replicated, may hold values from 0.5 to 1.5
- ffn_shift: float32 [768], replicated, may hold values from -3 to 3
- cotangent: bfloat16 [32, 512, 768], P(('batch', 'tensor')), may hold values from -6 to 6
Outputs:
- layer_out: bfloat16 [32, 512, 768], P(('batch', 'tensor'))
- pooled: float32 [32, 8, 768], P(('batch', 'tensor'))
- grad_input: float32 [32, 512, 768], P(('batch', 'tensor'))
- grad_query_weight: float32 [768, 768], P(None, 'tensor')
- grad_query_bias: float32 [768], P('tensor')
- grad_key_weight: float32 [768, 768], P(None, 'tensor')
- grad_value_weight: float32 [768, 768], P(None, 'tensor')
- grad_value_bias: float32 [768], P('tensor')
- grad_out_weight: float32 [768, 768], P('tensor')
- grad_out_bias: float32 [768], P('tensor')
- grad_attn_gain: float32 [768], P('tensor')
- grad_attn_shift: float32 [768], P('tensor')
- grad_up_weight: float32 [768, 3072], P(None, 'tensor')
- grad_up_bias: float32 [3072], P('tensor')
- grad_down_weight: float32 [3072, 768], P('tensor')
- grad_down_bias: float32 [768], P('tensor')
- grad_ffn_gain: float32 [768], P('tensor')
- grad_ffn_shift: float32 [768], P('tensor')
Inputs may be any that keep to these rules, and one draw needn't show every extreme that they name: `segment_ids`: in each row the text numbers never fall, every text 0 to 7 occurs, each has 1 to 128 positions, and some text has exactly 128.
All inputs are finite; a program needn't handle non-finite values.
Results may differ from a plain program's by a relative error of at most 0.015.
Values may be sent and summed in bfloat16 or wider, within the bound.
A program may use at most 128 MiB of HBM per device.

v0:
```python
import math
import jax
import jax.numpy as jnp
from jax import lax
from jax.sharding import PartitionSpec as P

HEAD_DIM = 64
TEXTS = 8


def product(left, right):
    return jnp.dot(left, right, preferred_element_type=jnp.float32)


def through_rows(left, right):
    return lax.dot_general(
        left, right, (((0,), (0,)), ((), ())), preferred_element_type=jnp.float32
    )


def against_cols(left, right):
    return lax.dot_general(
        left, right, (((1,), (1,)), ((), ())), preferred_element_type=jnp.float32
    )


def normalize(resid, gain, shift):
    center = resid - jnp.mean(resid, axis=-1, keepdims=True)
    spread = jnp.mean(center * center, axis=-1, keepdims=True)
    return center * lax.rsqrt(spread + 1e-12) * gain + shift


def gelu_exact(value):
    return jax.nn.gelu(value, approximate=False)


def per_device(
    hidden_in,
    segment_ids,
    query_weight,
    query_bias,
    key_weight,
    value_weight,
    value_bias,
    out_weight,
    out_bias,
    attn_gain,
    attn_shift,
    up_weight,
    up_bias,
    down_weight,
    down_bias,
    ffn_gain,
    ffn_shift,
    cotangent,
):
    local_rows, length, model_width = hidden_in.shape
    inner_width = query_weight.shape[1]
    heads_here = inner_width // HEAD_DIM
    score_scale = 1.0 / math.sqrt(HEAD_DIM)
    gathered = lax.all_gather(hidden_in, "tensor", axis=0, tiled=True)
    all_rows = gathered.shape[0]
    tokens = all_rows * length
    flat_in = gathered.reshape(tokens, model_width)
    query = (product(flat_in, query_weight) + query_bias).astype(jnp.bfloat16)
    keyset = product(flat_in, key_weight).astype(jnp.bfloat16)
    valueset = (product(flat_in, value_weight) + value_bias).astype(jnp.bfloat16)

    def by_heads(tensor):
        return tensor.reshape(all_rows, length, heads_here, HEAD_DIM)

    query_heads, key_heads, value_heads = (by_heads(query), by_heads(keyset), by_heads(valueset))

    def scored(query_row, key_row, segment_row):
        scores = (
            jnp.einsum("qhd,khd->hqk", query_row, key_row, preferred_element_type=jnp.float32)
            * score_scale
        )
        same_text = segment_row[:, None] == segment_row[None, :]
        return jnp.where(same_text[None], scores, -1000000000.0)

    def attend(items):
        query_row, key_row, value_row, segment_row = items
        scores = scored(query_row, key_row, segment_row)
        row_peak = jnp.max(scores, axis=-1, keepdims=True)
        exponent = jnp.exp(scores - row_peak)
        row_total = jnp.sum(exponent, axis=-1, keepdims=True)
        probability = (exponent / row_total).astype(jnp.bfloat16)
        context_row = jnp.einsum(
            "hqk,khd->qhd", probability, value_row, preferred_element_type=jnp.float32
        )
        return (context_row.astype(jnp.bfloat16), row_peak + jnp.log(row_total))

    context, log_totals = lax.map(attend, (query_heads, key_heads, value_heads, segment_ids))
    context = context.reshape(all_rows, length, inner_width)
    input_float = hidden_in.astype(jnp.float32)
    partial_out = product(context.reshape(tokens, inner_width), out_weight).reshape(
        all_rows, length, model_width
    )
    attn = lax.psum_scatter(partial_out, "tensor", scatter_dimension=0, tiled=True)
    hidden1, norm1_pull = jax.vjp(normalize, attn + out_bias + input_float, attn_gain, attn_shift)
    hidden1_low = hidden1.astype(jnp.bfloat16)
    hidden1_all = lax.all_gather(hidden1_low, "tensor", axis=0, tiled=True).reshape(
        tokens, model_width
    )
    preact = product(hidden1_all, up_weight) + up_bias
    activated, gelu_pull = jax.vjp(gelu_exact, preact)
    activated_low = activated.astype(jnp.bfloat16)
    partial_ffn = product(activated_low, down_weight).reshape(all_rows, length, model_width)
    ffn = lax.psum_scatter(partial_ffn, "tensor", scatter_dimension=0, tiled=True)
    final, norm2_pull = jax.vjp(normalize, ffn + down_bias + hidden1, ffn_gain, ffn_shift)
    first_row = lax.axis_index("tensor") * local_rows
    segment_here = lax.dynamic_slice_in_dim(segment_ids, first_row, local_rows, 0)
    labels = jnp.arange(TEXTS, dtype=jnp.int32)
    member = (segment_here[:, None, :] == labels[None, :, None]).astype(jnp.float32)
    counts = jnp.sum(member, axis=-1)
    pooled = (
        jnp.einsum("rts,rsd->rtd", member, final, precision=lax.Precision.HIGHEST)
        / counts[:, :, None]
    )
    dresid2, ffn_gain_part, ffn_shift_part = norm2_pull(cotangent.astype(jnp.float32))
    down_bias_part = jnp.sum(dresid2, axis=(0, 1))
    dffn_low = dresid2.astype(jnp.bfloat16)
    dffn_all = lax.all_gather(dffn_low, "tensor", axis=0, tiled=True).reshape(tokens, model_width)
    grad_down = through_rows(activated_low, dffn_all)
    dactivated = against_cols(dffn_all, down_weight)
    dpreact = gelu_pull(dactivated)[0].astype(jnp.bfloat16)
    grad_up_bias = jnp.sum(dpreact.astype(jnp.float32), axis=0)
    grad_up = through_rows(hidden1_all, dpreact)
    dhidden_part = against_cols(dpreact, up_weight).reshape(all_rows, length, model_width)
    dhidden1 = lax.psum_scatter(dhidden_part, "tensor", scatter_dimension=0, tiled=True) + dresid2
    dresid1, attn_gain_part, attn_shift_part = norm1_pull(dhidden1)
    out_bias_part = jnp.sum(dresid1, axis=(0, 1))
    dattn_low = dresid1.astype(jnp.bfloat16)
    dattn_all = lax.all_gather(dattn_low, "tensor", axis=0, tiled=True).reshape(tokens, model_width)
    grad_out = through_rows(context.reshape(tokens, inner_width), dattn_all)
    dcontext = against_cols(dattn_all, out_weight).astype(jnp.bfloat16)
    dcontext_heads = by_heads(dcontext)

    def attend_back(items):
        query_row, key_row, value_row, segment_row, log_row, dctx_row = items
        scores = scored(query_row, key_row, segment_row)
        probability = jnp.exp(scores - log_row)
        dvalue_row = jnp.einsum(
            "hqk,qhd->khd",
            probability.astype(jnp.bfloat16),
            dctx_row,
            preferred_element_type=jnp.float32,
        ).astype(jnp.bfloat16)
        dprobs = jnp.einsum("qhd,khd->hqk", dctx_row, value_row, preferred_element_type=jnp.float32)
        dscores = (
            probability * (dprobs - jnp.sum(dprobs * probability, axis=-1, keepdims=True))
        ).astype(jnp.bfloat16)
        dquery_row = (
            jnp.einsum("hqk,khd->qhd", dscores, key_row, preferred_element_type=jnp.float32)
            * score_scale
        ).astype(jnp.bfloat16)
        dkey_row = (
            jnp.einsum("hqk,qhd->khd", dscores, query_row, preferred_element_type=jnp.float32)
            * score_scale
        ).astype(jnp.bfloat16)
        return (dquery_row, dkey_row, dvalue_row)

    dquery, dkey, dvalue = lax.map(
        attend_back, (query_heads, key_heads, value_heads, segment_ids, log_totals, dcontext_heads)
    )
    dquery = dquery.reshape(tokens, inner_width)
    dkey = dkey.reshape(tokens, inner_width)
    dvalue = dvalue.reshape(tokens, inner_width)
    grad_query = through_rows(flat_in, dquery)
    grad_query_bias = jnp.sum(dquery.astype(jnp.float32), axis=0)
    grad_key = through_rows(flat_in, dkey)
    grad_value = through_rows(flat_in, dvalue)
    grad_value_bias = jnp.sum(dvalue.astype(jnp.float32), axis=0)
    dinput_part = (
        against_cols(dquery, query_weight)
        + against_cols(dkey, key_weight)
        + against_cols(dvalue, value_weight)
    ).reshape(all_rows, length, model_width)
    vector_terms = jnp.stack(
        [
            out_bias_part,
            attn_gain_part,
            attn_shift_part,
            down_bias_part,
            ffn_gain_part,
            ffn_shift_part,
        ]
    )
    dinput, vector_sums = (
        lax.psum_scatter(
            dinput_part.astype(jnp.bfloat16), "tensor", scatter_dimension=0, tiled=True
        ).astype(jnp.float32),
        lax.psum_scatter(
            vector_terms.astype(jnp.bfloat16), "tensor", scatter_dimension=1, tiled=True
        ).astype(jnp.float32),
    )
    totals = lax.psum(
        (
            grad_query,
            grad_query_bias,
            grad_key,
            grad_value,
            grad_value_bias,
            grad_out,
            grad_up,
            grad_up_bias,
            grad_down,
            vector_sums,
        ),
        "batch",
    )
    vectors = totals[9]
    return (
        final.astype(jnp.bfloat16),
        pooled,
        dinput + dresid1,
        totals[0],
        totals[1],
        totals[2],
        totals[3],
        totals[4],
        totals[5],
        vectors[0],
        vectors[1],
        vectors[2],
        totals[6],
        totals[7],
        totals[8],
        vectors[3],
        vectors[4],
        vectors[5],
    )


def solution(mesh):
    in_specs = (
        P(("batch", "tensor"), None, None),
        P("batch", None),
        P(None, "tensor"),
        P("tensor"),
        P(None, "tensor"),
        P(None, "tensor"),
        P("tensor"),
        P("tensor", None),
        P(),
        P(),
        P(),
        P(None, "tensor"),
        P("tensor"),
        P("tensor", None),
        P(),
        P(),
        P(),
        P(("batch", "tensor"), None, None),
    )
    out_specs = (
        P(("batch", "tensor"), None, None),
        P(("batch", "tensor"), None, None),
        P(("batch", "tensor"), None, None),
        P(None, "tensor"),
        P("tensor"),
        P(None, "tensor"),
        P(None, "tensor"),
        P("tensor"),
        P("tensor", None),
        P("tensor"),
        P("tensor"),
        P("tensor"),
        P(None, "tensor"),
        P("tensor"),
        P("tensor", None),
        P("tensor"),
        P("tensor"),
        P("tensor"),
    )
    return jax.shard_map(
        per_device, mesh=mesh, in_specs=in_specs, out_specs=out_specs, check_vma=False
    )
```

profile of v0, /device:TPU:0, one launch (start us, length us, event | category | flops | bytes accessed | tf_op | source)
XLA Modules:
  0.0 927.1 jit_solution(11372551995541683853)
XLA Ops:
  8.0 67.8 %all-gather.5.cloned.1.call-done = bf16[4,512,768]{2,1,0:T(8,128)(2,1)} async-done(((bf16[1,512,768]{2,1,0:T(8,128)(2,1)}), bf16[4,512,768]{2,1,0:T(8,128)(2,1)}) %all-gather.5.cloned.1.call-update) | async-done | bytes 3145744 | tf_op jit(solution)/shard_map/all_gather | solution.py:61
  75.8 3.2 fusion.60
  80.6 3.1 fusion.61
  84.6 3.1 convolution_convert_fusion.1
  88.5 17.4 %while.26 = (s32[]{:T(128)}, bf16[4,512,3,64]{1,3,2,0:T(8,128)(2,1)S(1)}, f32[4,3,512,1]{2,1,3,0:T(4,128)}, bf16[4,512,3,64]{1,3,2,0:T(8,128)(2,1)}, s32[4,512]{...) while((s32[]{:T(128)}, ...), condition=%wide.region_3.4_spmd, body=%wide.region_0.3_spmd.sunk | while | flops 211122688 | bytes 11336281 | solution.py:94
  90.8 2.0 fusion.154
  95.2 2.0 fusion.154
  99.5 2.0 fusion.154
  103.9 2.0 fusion.154
  105.9 4.9 fusion.81
  110.9 109.5 %reduce-scatter.8.cloned.1.call-done = f32[1,512,768]{2,1,0:T(8,128)} async-done(((f32[4,512,768]{2,1,0:T(8,128)}), f32[1,512,768]{2,1,0:T(8,128)}) %reduce-scatter.8.cloned.1.call-update) | async-done | bytes 1572880 | tf_op jit(solution)/shard_map/reduce_scatter | solution.py:100
  220.4 1.9 fusion.90
  223.8 1.9 fusion.68
  226.1 63.7 %all-gather.7.cloned.1.call-done = bf16[4,512,768]{2,1,0:T(8,128)(2,1)} async-done(((bf16[1,512,768]{2,1,0:T(8,128)(2,1)}), bf16[4,512,768]{2,1,0:T(8,128)(2,1)}) %all-gather.7.cloned.1.call-update) | async-done | bytes 3145744 | tf_op jit(solution)/shard_map/all_gather | solution.py:103
  289.8 18.4 %multiply_convert_fusion.1 = (bf16[2048,768]{1,0:T(8,128)(2,1)S(1)}, f32[2048,768]{1,0:T(8,128)}, f32[2048,768]{1,0:T(8,128)}) fusion(f32[768]{0:T(1024)} %param.34, bf16[2048,768]{1,0:T(8,128)(2,1)} %bitcast.240, bf16[768,768]{1,0:T(8,128)(2,1)S(1)} %copy-done), kind=kOutput, calls=%fused_computation.67 | convolution fusion | flops 2519728128 | bytes 20057088 | tf_op jit(solution)/shard_map/dot_general | solution.py:12
  308.3 4.5 fusion.92
  312.8 109.5 %reduce-scatter.10.cloned.1.call-done = f32[1,512,768]{2,1,0:T(8,128)} async-done(((f32[4,512,768]{2,1,0:T(8,128)}), f32[1,512,768]{2,1,0:T(8,128)}) %reduce-scatter.10.cloned.1.call-update) | async-done | bytes 1572880 | tf_op jit(solution)/shard_map/reduce_scatter | solution.py:110
  422.4 2.1 fusion.88
  424.8 1.3 fusion.65
  426.1 1.6 fusion.87
  427.8 1.1 copy-done.6
  428.9 1.7 add_reduce_fusion.1
  431.1 63.5 %all-gather.9.cloned.1.call-done = bf16[4,512,768]{2,1,0:T(8,128)(2,1)} async-done(((bf16[1,512,768]{2,1,0:T(8,128)(2,1)}), bf16[4,512,768]{2,1,0:T(8,128)(2,1)}) %all-gather.9.cloned.1.call-update) | async-done | bytes 3145744 | tf_op jit(solution)/shard_map/all_gather | solution.py:124
  494.7 11.0 %convert_reduce_fusion = (f32[768]{0:T(1024)}, bf16[2048,768]{1,0:T(8,128)(2,1)S(1)}) fusion(f32[2048,768]{1,0:T(8,128)} %get-tuple-element.242, f32[2048,768]{1,0:T(8,128)} %get-tuple-element.260, f32[768]{0:T(1024)} %param.34, bf16[2048,768]{1,0:T(8,128)(2,1)} %bitcast.242, bf16[768,768]{1,0:T(8,128)(2,1)} %param.35), kind=kOutput, calls=%fused_computation.64 | convolution fusion | flops 2442657024 | bytes 20060160 | tf_op jit(solution)/shard_map/dot_general | solution.py:22
  505.7 4.5 fusion.93
  510.3 109.5 %reduce-scatter.12.cloned.1.call-done = f32[1,512,768]{2,1,0:T(8,128)} async-done(((f32[4,512,768]{2,1,0:T(8,128)}), f32[1,512,768]{2,1,0:T(8,128)}) %reduce-scatter.12.cloned.1.call-update) | async-done | bytes 1572880 | tf_op jit(solution)/shard_map/reduce_scatter | solution.py:131
  619.8 2.7 multiply_reduce_fusion.1
  623.3 1.1 copy-done.5
  626.9 62.7 %all-gather.11.cloned.1.call-done = bf16[4,512,768]{2,1,0:T(8,128)(2,1)} async-done(((bf16[1,512,768]{2,1,0:T(8,128)(2,1)}), bf16[4,512,768]{2,1,0:T(8,128)(2,1)}) %all-gather.11.cloned.1.call-update) | async-done | bytes 3145744 | tf_op jit(solution)/shard_map/all_gather | solution.py:135
  689.6 3.1 convolution_convert_fusion
  695.4 29.0 %while.27 = (s32[]{:T(128)}, bf16[4,512,3,64]{1,3,2,0:T(8,128)(2,1)S(1)}, bf16[4,512,3,64]{1,3,2,0:T(8,128)(2,1)}, bf16[4,512,3,64]{1,3,2,0:T(8,128)(2,1)}, bf16...) while((s32[]{:T(128)}, ...), condition=%wide.region_18.19_spmd, body=%wide.region_16.18_spmd.sunk | while | flops 511146496 | bytes 26127476 | solution.py:164
  697.3 1.6 multiply_reduce_fusion.6
  699.7 1.3 fusion.164
  701.4 1.3 fusion.165
  704.6 1.6 multiply_reduce_fusion.6
  707.0 1.3 fusion.164
  708.6 1.3 fusion.165
  711.8 1.6 multiply_reduce_fusion.6
  714.2 1.3 fusion.164
  715.9 1.3 fusion.165
  719.1 1.6 multiply_reduce_fusion.6
  721.5 1.3 fusion.164
  723.2 1.3 fusion.165
  724.5 2.1 copy.90
  730.6 2.8 add_convert_fusion
  733.7 1.9 copy.91
  735.8 6.2 fusion.98
  742.0 4.2 fusion.97
  746.2 1.7 convolution_bitcast_fusion
  747.8 1.7 convolution_bitcast_fusion.1
  749.5 1.7 convolution_bitcast_fusion.2
  751.7 1.6 fusion.96
  753.5 1.2 copy-done.4
  754.7 1.5 fusion.73
  757.1 1.4 convert_reduce_fusion.1
  758.7 25.2 %all-reduce = (f32[192]{0:T(256)}, f32[192]{0:T(256)}, f32[6,192]{1,0:T(8,128)S(1)}, f32[768]{0:T(1024)}) all-reduce(f32[192]{0:T(256)S(1)} %reduce_sum.226, f32[192]{0:T(256)S(1)} %reduce_sum.228, bf16[6,192]{1,0:T(8,128)(2,1)S(1)} %copy.97, f32[768]{0:T(1024)S(1)} %copy-done.43), channel_id=1, replica_groups=mesh['batch'=8,'tensor'=4] {'batch'}, use_global_device_ids=true, to_apply=%region_22.23 | all-reduce | flops 2304 | bytes 16128 | tf_op jit(solution)/shard_map/psum | solution.py:198
  784.5 8.1 reduce-scatter.14.cloned.1.call-done
  792.7 3.0 convert_add_fusion
  795.7 114.8 %all-reduce.4.cloned.1.call-done = (f32[768,192]{0,1:T(8,128)}, f32[768,192]{0,1:T(8,128)}, f32[768,192]{0,1:T(8,128)}, f32[192,768]{1,0:T(8,128)}, f32[768,768]{1,0:T(8,128)}, /*index=5*/f32[768,768]{1,0:T(8,128)}) async-done(((f32[768,192]{0,1:T(8,128)}, f32[768,192]{0,1:T(8,128)}, f32[768,192]{0,1:T(8,128)}, f32[192,768]{1,0:T(8,128)}, f32[768,768]{1,0:T(8,128)}, /*index=5*/f32[768,768]{1,0:T(8,128)}), ...) | async-done | bytes 7077904 | tf_op jit(solution)/shard_map/psum | solution.py:198
  910.5 2.1 copy.135
  912.5 1.9 copy.136
  914.5 1.9 copy.137
  917.2 1.4 copy.139
  918.6 1.4 copy.140
  (215 shorter events, 42.1 us)
Async XLA Ops:
  7.2 282.6 %copy-start = (bf16[768,768]{1,0:T(8,128)(2,1)S(1)}, bf16[768,768]{1,0:T(8,128)(2,1)}, u32[]{:S(2)}) copy-start(bf16[768,768]{1,0:T(8,128)(2,1)} %param.33) | copy-start | bytes 3538948
  7.2 68.6 %all-gather.5.cloned.1.call-start = ((), (), s32[]{:S(2)}) async-start(), calls=%async_computation.5 | async-start | bytes 3932160 | tf_op jit(solution)/shard_map/all_gather | solution.py:61
  7.9 212.5 %reduce-scatter.8.cloned.1.call-start = ((), (), s32[]{:S(2)}) async-start(), calls=%async_computation.6 | async-start | bytes 7864320 | tf_op jit(solution)/shard_map/reduce_scatter | solution.py:100
  79.0 1.6 copy-start.20
  79.0 1.6 copy-start.48
  83.7 1.0 copy-start.22
  87.7 0.8 copy-start.26
  105.9 4.9 copy-start.7
  105.9 4.9 copy-start.11
  110.8 109.6 %copy-start.44 = (f32[768]{0:T(1024)S(1)}, f32[768]{0:T(1024)}, u32[]{:S(2)}) copy-start(f32[768]{0:T(1024)} %param.30) | copy-start | bytes 9220
  110.8 113.0 %copy-start.25 = (f32[768]{0:T(1024)S(1)}, f32[768]{0:T(1024)}, u32[]{:S(2)}) copy-start(f32[768]{0:T(1024)} %param.31) | copy-start | bytes 9220
  110.8 179.0 %all-gather.7.cloned.1.call-start = ((), (), s32[]{:S(2)}) async-start(), calls=%async_computation.7 | async-start | bytes 3932160 | tf_op jit(solution)/shard_map/all_gather | solution.py:103
  222.7 0.6 copy-start.35
  223.3 0.6 copy-start.27
  225.7 196.6 %reduce-scatter.10.cloned.1.call-start = ((), (), s32[]{:S(2)}) async-start(), calls=%async_computation.8 | async-start | bytes 7864320 | tf_op jit(solution)/shard_map/reduce_scatter | solution.py:110
  289.8 18.4 %copy-start.47 = (bf16[768,768]{1,0:T(8,128)(2,1)S(1)}, bf16[768,768]{1,0:T(8,128)(2,1)}, u32[]{:S(2)}) copy-start(bf16[768,768]{1,0:T(8,128)(2,1)} %param.35) | copy-start | bytes 3538948
  308.3 4.5 copy-start.49
  312.8 181.9 %all-gather.9.cloned.1.call-start = ((), (), s32[]{:S(2)}) async-start(), calls=%async_computation.9 | async-start | bytes 3932160 | tf_op jit(solution)/shard_map/all_gather | solution.py:124
  422.4 2.4 copy-start.12
  422.4 2.4 copy-start.37
  424.4 3.3 copy-start.3
  424.4 1.7 copy-start.41
  424.5 3.2 copy-start.29
  424.8 2.9 copy-start.31
  427.7 1.1 copy-start.6
  427.7 2.8 copy-start.33
  430.6 189.3 %reduce-scatter.12.cloned.1.call-start = ((), (), s32[]{:S(2)}) async-start(), calls=%async_computation.10 | async-start | bytes 7864320 | tf_op jit(solution)/shard_map/reduce_scatter | solution.py:131
  505.7 4.5 copy-start.50
  510.2 109.6 %copy-start.28 = (f32[512]{0:T(512)S(1)}, f32[512]{0:T(512)}, u32[]{:S(2)}) copy-start(f32[512]{0:T(512)} %copy-done.27) | copy-start | bytes 6148
  510.2 109.6 %copy-start.34 = (f32[512]{0:T(512)S(1)}, f32[512]{0:T(512)}, u32[]{:S(2)}) copy-start(f32[512]{0:T(512)} %copy-done.33) | copy-start | bytes 6148
  510.3 112.3 %copy-start.36 = (f32[512]{0:T(512)S(1)}, f32[512]{0:T(512)}, u32[]{:S(2)}) copy-start(f32[512]{0:T(512)} %copy-done.35) | copy-start | bytes 6148
  510.3 179.3 %all-gather.11.cloned.1.call-start = ((), (), s32[]{:S(2)}) async-start(), calls=%async_computation.11 | async-start | bytes 3932160 | tf_op jit(solution)/shard_map/all_gather | solution.py:135
  622.6 3.0 copy-start.13
  623.2 1.2 copy-start.5
  623.2 2.5 copy-start.40
  623.2 2.5 copy-start.39
  623.2 66.3 %copy-start.19 = (bf16[192,768]{1,0:T(8,128)(2,1)S(1)}, bf16[192,768]{1,0:T(8,128)(2,1)}, u32[]{:S(2)}) copy-start(bf16[192,768]{1,0:T(8,128)(2,1)} %param.29) | copy-start | bytes 884740
  625.5 130.8 %reduce-scatter.16.cloned.1.call-start = ((), (), s32[]{:S(2)}) async-start(), calls=%async_computation.13 | async-start | bytes 245760
  626.7 166.0 %reduce-scatter.14.cloned.1.call-start = ((), (), s32[]{:S(2)}) async-start(), calls=%async_computation.12 | async-start | bytes 3932160 | tf_op jit(solution)/shard_map/reduce_scatter | solution.py:191
  692.7 2.8 copy-start.8
  724.5 2.1 copy-start.9
  724.5 2.3 copy-start.15
  726.5 1.1 copy-start.10
  726.7 1.7 copy-start.21
  728.5 1.1 copy-start.23
  729.5 1.1 copy-start.24
  733.5 177.0 %all-reduce.4.cloned.1.call-start = ((), (), s32[]{:S(2)}) async-start(), calls=%async_computation.14 | async-start | bytes 14155776 | tf_op jit(solution)/shard_map/psum | solution.py:198
  733.7 2.1 copy-start.46
  735.8 6.2 copy-start.45
  735.8 6.2 copy-start.51
  742.0 4.2 copy-start.2
  749.5 2.2 copy-start.14
  753.3 1.4 copy-start.4
  753.3 1.4 copy-start.30
  753.3 1.4 copy-start.32
  753.3 1.4 copy-start.38
  753.3 1.4 copy-start.42
  753.4 5.4 copy-start.43
  910.5 5.9 copy-start.18
  910.5 6.7 copy-start.17
  916.4 2.2 copy-start.16
  917.2 2.8 copy-start.1
Sparse Core Ops, SparseCore 0:
  9.6 66.1 all-gather.4
  110.9 109.4 reduce-scatter.7
  225.9 63.9 all-gather.6
  312.9 109.4 reduce-scatter.9
  430.7 63.9 all-gather.8
  510.4 109.4 reduce-scatter.11
  625.6 63.9 all-gather.10
  691.8 18.2 reduce-scatter.15
  733.6 59.0 reduce-scatter.13
  797.7 112.7 all-reduce.3
where the time goes:
time: 935 us; the launch traced here: 927 us
  waiting for transfers between devices  710 us (76%)
  matrix products  112 us (12%)
  local copies, waits for them, and re-layouts  32.4 us (3%)
  other arithmetic  30.5 us (3%)
  blocking collectives  25.2 us (3%)
  between operations  15 us (2%)
    psum x1, waiting for transfers between devices, per_device(): lax.psum((grad_query, grad_query_bias, grad_key, grad_value, grad_value_b...  115 us
    reduce_scatter x1, waiting for transfers between devices, per_device(): lax.psum_scatter(partial_ffn, 'tensor', scatter_dimension=0, tiled=True)  110 us
    reduce_scatter x1, waiting for transfers between devices, per_device(): lax.psum_scatter(dhidden_part, 'tensor', scatter_dimension=0, tiled=True)  110 us
    reduce_scatter x1, waiting for transfers between devices, per_device(): lax.psum_scatter(partial_out, 'tensor', scatter_dimension=0, tiled=True)  110 us
    all_gather x1, waiting for transfers between devices, per_device(): gathered = lax.all_gather(hidden_in, 'tensor', axis=0, tiled=True)  67.8 us
    all_gather x1, waiting for transfers between devices, per_device(): lax.all_gather(hidden1_low, 'tensor', axis=0, tiled=True)  63.7 us
    all_gather x1, waiting for transfers between devices, per_device(): lax.all_gather(dffn_low, 'tensor', axis=0, tiled=True)  63.5 us
    all_gather x1, waiting for transfers between devices, per_device(): lax.all_gather(dattn_low, 'tensor', axis=0, tiled=True)  62.7 us
  transfers between devices with their start and end apart: 10, of which 9 were waited for; matrix products, arithmetic and copies ran while one was open for 8% of the time, Pallas kernels for 0%

commit v1 on v0

--- a/solution.py
+++ b/solution.py
@@ -1,3 +1,4 @@
+import functools
 import math
 import jax
 import jax.numpy as jnp
@@ -6,6 +7,37 @@
 
 HEAD_DIM = 64
 TEXTS = 8
+
+
+def lead_edge_over_axis(packet, at_axis):
+    packet = jnp.moveaxis(packet, 0, at_axis)
+    front = packet.shape
+    return packet.reshape(
+        *front[:at_axis], front[at_axis] * front[at_axis + 1], *front[at_axis + 2 :]
+    )
+
+
+def get_turns(xx, ndim_at, bus_axis):
+    lanes = []
+    num_devices = lax.psum(1, bus_axis)
+    for at in range(num_devices):
+        lanes.append((at, (at + 1) % num_devices))
+    arrivals = []
+    for k0, c in lanes:
+        arrivals.append((c, k0))
+    u1, high = ([], [])
+    for s in range(num_devices - 1):
+        if s % 2 == 0:
+            u1.append(lax.ppermute(u1[-1] if u1 else xx, bus_axis, lanes))
+        else:
+            high.append(lax.ppermute(high[-1] if high else xx, bus_axis, arrivals))
+    big = jnp.stack([*u1[::-1], xx, *high])
+    prior = lax.axis_index(bus_axis) - len(u1)
+    big = big[(jnp.arange(num_devices) - prior) % num_devices]
+    return lead_edge_over_axis(big, ndim_at)
+
+
+take_the_views = functools.partial(get_turns, ndim_at=0, bus_axis="tensor")
 
 
 def product(left, right):
@@ -121,7 +153,7 @@
     dresid2, ffn_gain_part, ffn_shift_part = norm2_pull(cotangent.astype(jnp.float32))
     down_bias_part = jnp.sum(dresid2, axis=(0, 1))
     dffn_low = dresid2.astype(jnp.bfloat16)
-    dffn_all = lax.all_gather(dffn_low, "tensor", axis=0, tiled=True).reshape(tokens, model_width)
+    dffn_all = take_the_views(dffn_low).reshape(tokens, model_width)
     grad_down = through_rows(activated_low, dffn_all)
     dactivated = against_cols(dffn_all, down_weight)
     dpreact = gelu_pull(dactivated)[0].astype(jnp.bfloat16)

time: 935 us -> 934 us (level)
  waiting for transfers between devices: 710 us -> 683 us
  starting transfers between devices: 1.61 us -> 19.9 us
    all_gather x1 -> x0, waiting for transfers between devices: 63.5 us -> none  [per_device(): lax.all_gather(dffn_low, 'tensor', axis=0, tiled=True)]
    ppermute x0 -> x3, waiting for transfers between devices: none -> 35.6 us  [the longest x2 35.1 us: get_turns(): u1.append(lax.ppermute(u1[-1] if u1 else xx, bus_axis, lanes))]
    ppermute x0 -> x3, starting transfers between devices: none -> 18.8 us  [the longest x2 16.5 us: get_turns(): u1.append(lax.ppermute(u1[-1] if u1 else xx, bus_axis, lanes))]
  transfers between devices with their start and end apart: 10 -> 12, of which waited for: 9 -> 11; matrix products, arithmetic and copies ran while one was open for 8% -> 8% of each run, Pallas kernels for 0% -> 0%
where the time goes in v1:
time: 934 us; the launch traced here: 926 us
  waiting for transfers between devices  683 us (73%)
  matrix products  112 us (12%)
  local copies, waits for them, and re-layouts  36.6 us (4%)
  other arithmetic  34.4 us (4%)
  blocking collectives  25.2 us (3%)
  starting transfers between devices  19.9 us (2%)
  between operations  14.7 us (2%)
    psum x1, waiting for transfers between devices, per_device(): lax.psum((grad_query, grad_query_bias, grad_key, grad_value, grad_value_b...  115 us
    reduce_scatter x1, waiting for transfers between devices, per_device(): lax.psum_scatter(dhidden_part, 'tensor', scatter_dimension=0, tiled=True)  110 us
    reduce_scatter x1, waiting for transfers between devices, per_device(): lax.psum_scatter(partial_ffn, 'tensor', scatter_dimension=0, tiled=True)  110 us
    reduce_scatter x1, waiting for transfers between devices, per_device(): lax.psum_scatter(partial_out, 'tensor', scatter_dimension=0, tiled=True)  110 us
    all_gather x1, waiting for transfers between devices, per_device(): gathered = lax.all_gather(hidden_in, 'tensor', axis=0, tiled=True)  67.8 us
    all_gather x1, waiting for transfers between devices, per_device(): lax.all_gather(hidden1_low, 'tensor', axis=0, tiled=True)  63.7 us
    all_gather x1, waiting for transfers between devices, per_device(): lax.all_gather(dattn_low, 'tensor', axis=0, tiled=True)  62.7 us
    dot_general x6, matrix products, product(): return jnp.dot(left, right, preferred_element_type=jnp.float32)  37.1 us
  transfers between devices with their start and end apart: 12, of which 11 were waited for; matrix products, arithmetic and copies ran while one was open for 8% of the time, Pallas kernels for 0%

profile of v1, /device:TPU:0, one launch (start us, length us, event | category | flops | bytes accessed | tf_op | source)
XLA Modules:
  0.0 925.9 jit_solution(2860677074714312913)
XLA Ops:
  8.0 67.8 %all-gather.4.cloned.1.call-done = bf16[4,512,768]{2,1,0:T(8,128)(2,1)} async-done(((bf16[1,512,768]{2,1,0:T(8,128)(2,1)}), bf16[4,512,768]{2,1,0:T(8,128)(2,1)}) %all-gather.4.cloned.1.call-update) | async-done | bytes 3145744 | tf_op jit(solution)/shard_map/all_gather | solution.py:93
  75.8 3.2 fusion.60
  80.6 3.1 fusion.61
  84.4 3.1 convolution_convert_fusion.1
  88.3 17.4 %while.26 = (s32[]{:T(128)}, bf16[4,512,3,64]{1,3,2,0:T(8,128)(2,1)S(1)}, f32[4,3,512,1]{2,1,3,0:T(4,128)}, bf16[4,512,3,64]{1,3,2,0:T(8,128)(2,1)}, s32[4,512]{...) while((s32[]{:T(128)}, ...), condition=%wide.region_3.4_spmd, body=%wide.region_0.3_spmd.sunk | while | flops 211122688 | bytes 11336281 | solution.py:126
  90.6 2.0 fusion.156
  95.0 2.0 fusion.156
  99.3 2.0 fusion.156
  103.7 2.0 fusion.156
  105.7 4.9 fusion.81
  110.7 109.5 %reduce-scatter.8.cloned.1.call-done = f32[1,512,768]{2,1,0:T(8,128)} async-done(((f32[4,512,768]{2,1,0:T(8,128)}), f32[1,512,768]{2,1,0:T(8,128)}) %reduce-scatter.8.cloned.1.call-update) | async-done | bytes 1572880 | tf_op jit(solution)/shard_map/reduce_scatter | solution.py:132
  220.2 1.9 fusion.92
  223.6 1.9 fusion.68
  225.9 63.7 %all-gather.6.cloned.1.call-done = bf16[4,512,768]{2,1,0:T(8,128)(2,1)} async-done(((bf16[1,512,768]{2,1,0:T(8,128)(2,1)}), bf16[4,512,768]{2,1,0:T(8,128)(2,1)}) %all-gather.6.cloned.1.call-update) | async-done | bytes 3145744 | tf_op jit(solution)/shard_map/all_gather | solution.py:135
  289.6 18.4 %multiply_convert_fusion.1 = (bf16[2048,768]{1,0:T(8,128)(2,1)S(1)}, f32[2048,768]{1,0:T(8,128)}, f32[2048,768]{1,0:T(8,128)}) fusion(f32[768]{0:T(1024)} %param.34, bf16[2048,768]{1,0:T(8,128)(2,1)} %bitcast.250, bf16[768,768]{1,0:T(8,128)(2,1)S(1)} %copy-done), kind=kOutput, calls=%fused_computation.68 | convolution fusion | flops 2519728128 | bytes 20057088 | tf_op jit(solution)/shard_map/dot_general | solution.py:44
  308.1 4.5 fusion.94
  312.6 109.5 %reduce-scatter.10.cloned.1.call-done = f32[1,512,768]{2,1,0:T(8,128)} async-done(((f32[4,512,768]{2,1,0:T(8,128)}), f32[1,512,768]{2,1,0:T(8,128)}) %reduce-scatter.10.cloned.1.call-update) | async-done | bytes 1572880 | tf_op jit(solution)/shard_map/reduce_scatter | solution.py:142
  422.1 2.1 fusion.90
  425.9 1.6 fusion.89
  428.6 1.7 add_reduce_fusion.1
  430.3 1.5 collective-permute-start
  431.8 2.4 collective-permute-start.2
  434.1 18.7 %collective-permute-done = bf16[1,512,768]{2,1,0:T(8,128)(2,1)} collective-permute-done((bf16[1,512,768]{2,1,0:T(8,128)(2,1)}, bf16[1,512,768]{2,1,0:T(8,128)(2,1)}, u32[]{:S(2)}, u32[]{:S(2)}) %collective-permute-start) | collective-permute-done | bytes 786464 | tf_op jit(solution)/shard_map/ppermute | solution.py:31
  452.9 15.0 %collective-permute-start.1 = (bf16[1,512,768]{2,1,0:T(8,128)(2,1)}, bf16[1,512,768]{2,1,0:T(8,128)(2,1)}, u32[]{:S(2)}, u32[]{:S(2)}) collective-permute-start(bf16[1,512,768]{2,1,0:T(8,128)(2,1)} %collective-permute-done), channel_id=1, source_target_pairs={{0,1},{1,2},{2,3},{3,0},{4,5},{5,6},{6,7},{7,4},{8,9},{9,10},{10,1... | collective-permute-start | bytes 2359304 | tf_op jit(solution)/shard_map/ppermute | solution.py:31
  469.1 16.3 %collective-permute-done.1 = bf16[1,512,768]{2,1,0:T(8,128)(2,1)} collective-permute-done((bf16[1,512,768]{2,1,0:T(8,128)(2,1)}, bf16[1,512,768]{2,1,0:T(8,128)(2,1)}, u32[]{:S(2)}, u32[]{:S(2)}) %collective-permute-start.1) | collective-permute-done | bytes 786464 | tf_op jit(solution)/shard_map/ppermute | solution.py:31
  485.4 3.3 maximum_bitcast_fusion
  488.7 4.4 gather_fusion
  493.1 11.0 %convert_reduce_fusion = (f32[768]{0:T(1024)}, bf16[2048,768]{1,0:T(8,128)(2,1)S(1)}) fusion(f32[2048,768]{1,0:T(8,128)} %get-tuple-element.242, f32[2048,768]{1,0:T(8,128)} %get-tuple-element.260, f32[768]{0:T(1024)} %param.34, bf16[2048,768]{1,0:T(8,128)(2,1)} %bitcast.229, bf16[768,768]{1,0:T(8,128)(2,1)} %param.35), kind=kOutput, calls=%fused_computation.65 | convolution fusion | flops 2442657024 | bytes 20060160 | tf_op jit(solution)/shard_map/dot_general | solution.py:54
  504.1 4.5 fusion.95
  508.7 110.0 %reduce-scatter.12.cloned.1.call-done = f32[1,512,768]{2,1,0:T(8,128)} async-done(((f32[4,512,768]{2,1,0:T(8,128)}), f32[1,512,768]{2,1,0:T(8,128)}) %reduce-scatter.12.cloned.1.call-update) | async-done | bytes 1572880 | tf_op jit(solution)/shard_map/reduce_scatter | solution.py:163
  618.7 2.7 multiply_reduce_fusion.1
  625.8 62.7 %all-gather.8.cloned.1.call-done = bf16[4,512,768]{2,1,0:T(8,128)(2,1)} async-done(((bf16[1,512,768]{2,1,0:T(8,128)(2,1)}), bf16[4,512,768]{2,1,0:T(8,128)(2,1)}) %all-gather.8.cloned.1.call-update) | async-done | bytes 3145744 | tf_op jit(solution)/shard_map/all_gather | solution.py:167
  688.5 3.0 convolution_convert_fusion
  694.3 29.1 %while.27 = (s32[]{:T(128)}, bf16[4,512,3,64]{1,3,2,0:T(8,128)(2,1)S(1)}, bf16[4,512,3,64]{1,3,2,0:T(8,128)(2,1)}, bf16[4,512,3,64]{1,3,2,0:T(8,128)(2,1)}, bf16...) while((s32[]{:T(128)}, ...), condition=%wide.region_18.19_spmd, body=%wide.region_16.18_spmd.sunk | while | flops 511146496 | bytes 26127476 | solution.py:196
  696.2 1.6 multiply_reduce_fusion.6
  698.6 1.3 fusion.166
  700.3 1.3 fusion.167
  703.5 1.6 multiply_reduce_fusion.6
  707.5 1.3 fusion.167
  710.7 1.6 multiply_reduce_fusion.6
  713.1 1.3 fusion.166
  714.8 1.3 fusion.167
  718.0 1.6 multiply_reduce_fusion.6
  722.1 1.3 fusion.167
  723.4 2.1 copy.90
  729.6 2.8 add_convert_fusion
  732.7 1.9 copy.91
  734.8 6.2 fusion.100
  741.0 4.2 fusion.99
  745.1 1.7 convolution_bitcast_fusion
  746.8 1.7 convolution_bitcast_fusion.1
  748.4 1.7 convolution_bitcast_fusion.2
  750.6 1.6 fusion.98
  753.7 1.5 fusion.73
  756.1 1.4 convert_reduce_fusion.1
  757.7 25.2 %all-reduce = (f32[192]{0:T(256)}, f32[192]{0:T(256)}, f32[6,192]{1,0:T(8,128)S(1)}, f32[768]{0:T(1024)}) all-reduce(f32[192]{0:T(256)S(1)} %reduce_sum.226, f32[192]{0:T(256)S(1)} %reduce_sum.228, bf16[6,192]{1,0:T(8,128)(2,1)S(1)} %copy.97, f32[768]{0:T(1024)S(1)} %copy-done.43), channel_id=1, replica_groups=mesh['batch'=8,'tensor'=4] {'batch'}, use_global_device_ids=true, to_apply=%region_22.23 | all-reduce | flops 2304 | bytes 16128 | tf_op jit(solution)/shard_map/psum | solution.py:230
  783.5 8.2 reduce-scatter.14.cloned.1.call-done
  791.6 3.0 convert_add_fusion
  794.6 114.9 %all-reduce.4.cloned.1.call-done = (f32[768,192]{0,1:T(8,128)}, f32[768,192]{0,1:T(8,128)}, f32[768,192]{0,1:T(8,128)}, f32[192,768]{1,0:T(8,128)}, f32[768,768]{1,0:T(8,128)}, /*index=5*/f32[768,768]{1,0:T(8,128)}) async-done(((f32[768,192]{0,1:T(8,128)}, f32[768,192]{0,1:T(8,128)}, f32[768,192]{0,1:T(8,128)}, f32[192,768]{1,0:T(8,128)}, f32[768,768]{1,0:T(8,128)}, /*index=5*/f32[768,768]{1,0:T(8,128)}), ...) | async-done | bytes 7077904 | tf_op jit(solution)/shard_map/psum | solution.py:230
  909.6 2.1 copy.135
  911.6 1.9 copy.136
  913.6 1.9 copy.137
  916.3 1.4 copy.139
  917.7 1.4 copy.140
  (220 shorter events, 49.8 us)
Async XLA Ops:
  7.2 282.4 %copy-start = (bf16[768,768]{1,0:T(8,128)(2,1)S(1)}, bf16[768,768]{1,0:T(8,128)(2,1)}, u32[]{:S(2)}) copy-start(bf16[768,768]{1,0:T(8,128)(2,1)} %param.33) | copy-start | bytes 3538948
  7.2 68.6 %all-gather.4.cloned.1.call-start = ((), (), s32[]{:S(2)}) async-start(), calls=%async_computation.5 | async-start | bytes 3932160 | tf_op jit(solution)/shard_map/all_gather | solution.py:93
  7.9 212.3 %reduce-scatter.8.cloned.1.call-start = ((), (), s32[]{:S(2)}) async-start(), calls=%async_computation.6 | async-start | bytes 7864320 | tf_op jit(solution)/shard_map/reduce_scatter | solution.py:132
  79.0 1.6 copy-start.21
  79.0 1.6 copy-start.47
  87.5 0.8 copy-start.26
  105.7 4.9 copy-start.7
  105.7 4.9 copy-start.11
  110.6 109.6 %copy-start.44 = (f32[768]{0:T(1024)S(1)}, f32[768]{0:T(1024)}, u32[]{:S(2)}) copy-start(f32[768]{0:T(1024)} %param.30) | copy-start | bytes 9220
  110.6 113.0 %copy-start.25 = (f32[768]{0:T(1024)S(1)}, f32[768]{0:T(1024)}, u32[]{:S(2)}) copy-start(f32[768]{0:T(1024)} %param.31) | copy-start | bytes 9220
  110.6 179.0 %all-gather.6.cloned.1.call-start = ((), (), s32[]{:S(2)}) async-start(), calls=%async_computation.7 | async-start | bytes 3932160 | tf_op jit(solution)/shard_map/all_gather | solution.py:135
  222.4 0.6 copy-start.35
  223.1 0.6 copy-start.27
  225.5 196.6 %reduce-scatter.10.cloned.1.call-start = ((), (), s32[]{:S(2)}) async-start(), calls=%async_computation.8 | async-start | bytes 7864320 | tf_op jit(solution)/shard_map/reduce_scatter | solution.py:142
  289.6 18.4 %copy-start.46 = (bf16[768,768]{1,0:T(8,128)(2,1)S(1)}, bf16[768,768]{1,0:T(8,128)(2,1)}, u32[]{:S(2)}) copy-start(bf16[768,768]{1,0:T(8,128)(2,1)} %param.35) | copy-start | bytes 3538948
  308.1 4.5 copy-start.48
  312.5 306.2 %reduce-scatter.12.cloned.1.call-start = ((), (), s32[]{:S(2)}) async-start(), calls=%async_computation.9 | async-start | bytes 7864320 | tf_op jit(solution)/shard_map/reduce_scatter | solution.py:163
  422.1 2.4 copy-start.12
  422.1 2.4 copy-start.37
  424.2 3.3 copy-start.3
  424.2 1.7 copy-start.41
  424.2 3.2 copy-start.29
  424.6 2.9 copy-start.31
  427.5 1.1 copy-start.6
  427.5 2.8 copy-start.33
  430.3 22.6 %collective-permute-start = (bf16[1,512,768]{2,1,0:T(8,128)(2,1)}, bf16[1,512,768]{2,1,0:T(8,128)(2,1)}, u32[]{:S(2)}, u32[]{:S(2)}) collective-permute-start(bf16[1,512,768]{2,1,0:T(8,128)(2,1)} %get-tuple-element.251), channel_id=1, source_target_pairs={{0,1},{1,2},{2,3},{3,0},{4,5},{5,6},{6,7},{7,4},{8,9},{9,10},{10,1... | collective-permute-start | bytes 2359304 | tf_op jit(solution)/shard_map/ppermute | solution.py:31
  431.8 37.3 %collective-permute-start.2 = (bf16[1,512,768]{2,1,0:T(8,128)(2,1)}, bf16[1,512,768]{2,1,0:T(8,128)(2,1)}, u32[]{:S(2)}, u32[]{:S(2)}) collective-permute-start(bf16[1,512,768]{2,1,0:T(8,128)(2,1)} %get-tuple-element.251), channel_id=1, source_target_pairs={{1,0},{2,1},{3,2},{0,3},{5,4},{6,5},{7,6},{4,7},{9,8},{10,9},{11,1... | collective-permute-start | bytes 2359304 | tf_op jit(solution)/shard_map/ppermute | solution.py:33
  452.9 32.5 %collective-permute-start.1 = (bf16[1,512,768]{2,1,0:T(8,128)(2,1)}, bf16[1,512,768]{2,1,0:T(8,128)(2,1)}, u32[]{:S(2)}, u32[]{:S(2)}) collective-permute-start(bf16[1,512,768]{2,1,0:T(8,128)(2,1)} %collective-permute-done), channel_id=1, source_target_pairs={{0,1},{1,2},{2,3},{3,0},{4,5},{5,6},{6,7},{7,4},{8,9},{9,10},{10,1... | collective-permute-start | bytes 2359304 | tf_op jit(solution)/shard_map/ppermute | solution.py:31
  504.1 4.5 copy-start.49
  508.6 110.1 %copy-start.28 = (f32[512]{0:T(512)S(1)}, f32[512]{0:T(512)}, u32[]{:S(2)}) copy-start(f32[512]{0:T(512)} %copy-done.27) | copy-start | bytes 6148
  508.6 110.1 %copy-start.34 = (f32[512]{0:T(512)S(1)}, f32[512]{0:T(512)}, u32[]{:S(2)}) copy-start(f32[512]{0:T(512)} %copy-done.33) | copy-start | bytes 6148
  508.7 112.8 %copy-start.36 = (f32[512]{0:T(512)S(1)}, f32[512]{0:T(512)}, u32[]{:S(2)}) copy-start(f32[512]{0:T(512)} %copy-done.35) | copy-start | bytes 6148
  508.7 179.8 %all-gather.8.cloned.1.call-start = ((), (), s32[]{:S(2)}) async-start(), calls=%async_computation.10 | async-start | bytes 3932160 | tf_op jit(solution)/shard_map/all_gather | solution.py:167
  621.4 3.0 copy-start.13
  622.1 1.2 copy-start.5
  622.1 2.5 copy-start.40
  622.1 2.5 copy-start.39
  622.1 66.4 %copy-start.20 = (bf16[192,768]{1,0:T(8,128)(2,1)S(1)}, bf16[192,768]{1,0:T(8,128)(2,1)}, u32[]{:S(2)}) copy-start(bf16[192,768]{1,0:T(8,128)(2,1)} %param.29) | copy-start | bytes 884740
  624.4 130.8 %reduce-scatter.16.cloned.1.call-start = ((), (), s32[]{:S(2)}) async-start(), calls=%async_computation.12 | async-start | bytes 245760
  625.6 166.0 %reduce-scatter.14.cloned.1.call-start = ((), (), s32[]{:S(2)}) async-start(), calls=%async_computation.11 | async-start | bytes 3932160 | tf_op jit(solution)/shard_map/reduce_scatter | solution.py:223
  691.6 2.8 copy-start.8
  723.4 2.1 copy-start.9
  723.4 2.3 copy-start.16
  725.5 1.1 copy-start.10
  725.7 1.7 copy-start.22
  727.4 1.1 copy-start.23
  728.5 1.1 copy-start.24
  732.4 177.2 %all-reduce.4.cloned.1.call-start = ((), (), s32[]{:S(2)}) async-start(), calls=%async_computation.13 | async-start | bytes 14155776 | tf_op jit(solution)/shard_map/psum | solution.py:230
  732.7 2.1 copy-start.14
  734.8 6.2 copy-start.45
  734.8 6.2 copy-start.50
  741.0 4.2 copy-start.2
  748.4 2.2 copy-start.15
  752.2 1.4 copy-start.4
  752.2 1.4 copy-start.30
  752.2 1.4 copy-start.32
  752.2 1.4 copy-start.38
  752.3 1.4 copy-start.42
  752.3 5.4 copy-start.43
  909.6 5.9 copy-start.19
  909.6 6.7 copy-start.18
  915.5 2.2 copy-start.17
  916.3 2.8 copy-start.1
Sparse Core Ops, SparseCore 0:
  9.6 66.1 all-gather.3
  110.7 109.4 reduce-scatter.7
  225.7 63.9 all-gather.5
  312.7 109.4 reduce-scatter.9
  508.8 109.8 reduce-scatter.11
  624.5 63.9 all-gather.7
  690.7 18.2 reduce-scatter.15
  732.5 59.0 reduce-scatter.13
  796.8 112.6 all-reduce.3
